TPU v7x, 32 devices: a whole 2x2x4 slice. The times are simulated.
32 devices in a mesh: dp: 8 (over z, y), mp: 4 (over x, core).
Axes of the slice: x: 2, y: 2, z: 4, core: 2. Of those that a mesh axis runs over, the one named last changes fastest.
Arguments:
- prefix_hidden: bfloat16 [32, 1024, 2048], P(('dp', 'mp')), may hold values from -6 to 6
- prefix_len: int32 [32], P('dp'), may hold values from 256 to 1024
- actions: float32 [32, 50, 32], P('dp'), may hold values from -6 to 6
- noise: float32 [32, 50, 32], P('dp'), may hold values from -6 to 6
- time_index: int32 [32], P('dp'), may hold values from 0 to 999
- prefix_gain: float32 [2048], replicated, may hold values from 0.25 to 1.75
- key_weight: bfloat16 [2048, 256], P('dp'), may hold values from -0.125 to 0.125
- value_weight: bfloat16 [2048, 256], P('dp'), may hold values from -0.125 to 0.125
- action_in: bfloat16 [32, 1024], replicated, may hold values from -1 to 1
- attn_gain: float32 [1024], replicated, may hold values from 0.25 to 1.75
- query_w: bfloat16 [1024, 2048], P('dp', 'mp'), may hold values from -0.1875 to 0.1875
- akey_w: bfloat16 [1024, 256], P('dp'), may hold values from -0.1875 to 0.1875
- avalue_w: bfloat16 [1024, 256], P('dp'), may hold values from -0.1875 to 0.1875
- out_w: bfloat16 [2048, 1024], P('mp', 'dp'), may hold values from -0.125 to 0.125
- mlp_gain: float32 [1024], replicated, may hold values from 0.25 to 1.75
- gate_w: bfloat16 [1024, 4096], P('dp', 'mp'), may hold values from -0.1875 to 0.1875
- up_w: bfloat16 [1024, 4096], P('dp', 'mp'), may hold values from -0.1875 to 0.1875
- down_w: bfloat16 [4096, 1024], P('mp', 'dp'), may hold values from -0.09375 to 0.09375
- final_gain: float32 [1024], replicated, may hold values from 0.25 to 1.75
- head_w: bfloat16 [1024, 32], replicated, may hold values from -0.1875 to 0.1875
Outputs:
- velocity: float32 [32, 50, 32], P(('dp', 'mp'))
- ep_loss: float32 [32], P(('dp', 'mp'))
Inputs may be any that keep to these rules, and one draw needn't show every extreme that they name: `prefix_len`: prefix positions at or above an episode's length are padding that no output reads.
All inputs are finite; a program needn't handle non-finite values.
Results may differ from a plain program's by a relative error of at most 0.009.
Values may be sent and summed in bfloat16 or wider, within the bound.
No kernel may reach another device: no remote copies, remote signals or barrier semaphores. Data moves between devices by JAX's collectives and lax.ppermute only.
A program may use at most 64 MiB of HBM per device.

v0:
```python
import math
import jax
import jax.numpy as jnp
from jax import lax
from jax.sharding import PartitionSpec as P

TSTEPS = 1000


def rms(values, gain):
    return values * lax.rsqrt(jnp.mean(values * values, axis=-1, keepdims=True) + 1e-06) * gain


def time_embed(times, width):
    half = width // 2
    steps = jnp.arange(half, dtype=jnp.float32)
    period = 0.004 * jnp.power(jnp.float32(1000.0), steps / (half - 1))
    angle = times[:, None] * (2.0 * math.pi) / period[None, :]
    return jnp.concatenate([jnp.sin(angle), jnp.cos(angle)], axis=-1)


def attend(query, pkeys, pvals, akeys, avals, lengths):
    live = jnp.arange(pkeys.shape[1], dtype=jnp.int32)[None, :] < lengths[:, None]
    scores = jnp.einsum("erd,epd->erp", query, pkeys, preferred_element_type=jnp.float32)
    probs = jnp.where(live[:, None, :], jnp.exp(scores), 0.0)
    action_scores = jnp.einsum("erd,ecd->erc", query, akeys, preferred_element_type=jnp.float32)
    action_probs = jnp.exp(action_scores)
    denom = jnp.sum(probs, axis=-1) + jnp.sum(action_probs, axis=-1)
    weighted = jnp.einsum(
        "erp,epd->erd", probs.astype(jnp.bfloat16), pvals, preferred_element_type=jnp.float32
    )
    weighted = weighted + jnp.einsum(
        "erc,ecd->erd", action_probs.astype(jnp.bfloat16), avals, preferred_element_type=jnp.float32
    )
    return (weighted / denom[:, :, None]).astype(jnp.bfloat16)


def on_device(
    prefix_hidden,
    prefix_len,
    actions,
    noise,
    time_index,
    prefix_gain,
    key_weight,
    value_weight,
    action_in,
    attn_gain,
    query_w,
    akey_w,
    avalue_w,
    out_w,
    mlp_gain,
    gate_w,
    up_w,
    down_w,
    final_gain,
    head_w,
):
    own_eps, positions, width = prefix_hidden.shape
    group_eps, span, adim = actions.shape
    expert = action_in.shape[1]
    head_size = key_weight.shape[1]
    local_heads = query_w.shape[1] // head_size
    rows_total = group_eps * span
    own_rows = own_eps * span
    member = lax.axis_index("mp")
    first_row = member * own_rows
    first_ep = member * own_eps
    times = (time_index.astype(jnp.float32) + 0.5) / TSTEPS
    x_t = times[:, None, None] * noise + (1.0 - times)[:, None, None] * actions
    target = noise - actions
    x_in = x_t.reshape(rows_total, adim).astype(jnp.bfloat16)
    temb = time_embed(times, expert)
    h0 = (
        jnp.dot(x_in, action_in, preferred_element_type=jnp.float32).reshape(
            group_eps, span, expert
        )
        + temb[:, None, :]
    )
    h0 = h0.reshape(rows_total, expert)
    key_full, value_full = (
        lax.all_gather(key_weight, "dp", axis=0, tiled=True),
        lax.all_gather(value_weight, "dp", axis=0, tiled=True),
    )
    prefix_normed = rms(
        prefix_hidden.reshape(own_eps * positions, width).astype(jnp.float32), prefix_gain
    ).astype(jnp.bfloat16)
    pkeys = (
        jnp.dot(prefix_normed, key_full, preferred_element_type=jnp.float32)
        .astype(jnp.bfloat16)
        .reshape(own_eps, positions, head_size)
    )
    pvals = (
        jnp.dot(prefix_normed, value_full, preferred_element_type=jnp.float32)
        .astype(jnp.bfloat16)
        .reshape(own_eps, positions, head_size)
    )
    normed = rms(h0, attn_gain).astype(jnp.bfloat16)
    query_full, akey_full, avalue_full = (
        lax.all_gather(query_w, "dp", axis=0, tiled=True),
        lax.all_gather(akey_w, "dp", axis=0, tiled=True),
        lax.all_gather(avalue_w, "dp", axis=0, tiled=True),
    )
    query = (
        jnp.dot(normed, query_full, preferred_element_type=jnp.float32) * head_size ** (-0.5)
    ).astype(jnp.bfloat16)
    akeys = (
        jnp.dot(normed, akey_full, preferred_element_type=jnp.float32)
        .astype(jnp.bfloat16)
        .reshape(group_eps, span, head_size)
    )
    avals = (
        jnp.dot(normed, avalue_full, preferred_element_type=jnp.float32)
        .astype(jnp.bfloat16)
        .reshape(group_eps, span, head_size)
    )
    keys_all, vals_all = (
        lax.all_gather(pkeys, "mp", axis=0, tiled=True),
        lax.all_gather(pvals, "mp", axis=0, tiled=True),
    )
    attn = attend(
        query.reshape(group_eps, span * local_heads, head_size),
        keys_all,
        vals_all,
        akeys,
        avals,
        prefix_len,
    )
    attn = attn.reshape(rows_total, local_heads * head_size)
    out_full = lax.all_gather(out_w, "dp", axis=1, tiled=True)
    gate_full, up_full = (
        lax.all_gather(gate_w, "dp", axis=0, tiled=True),
        lax.all_gather(up_w, "dp", axis=0, tiled=True),
    )
    down_full = lax.all_gather(down_w, "dp", axis=1, tiled=True)
    h0_own = lax.dynamic_slice_in_dim(h0, first_row, own_rows, 0)
    h1 = h0_own + lax.psum_scatter(
        jnp.dot(attn, out_full, preferred_element_type=jnp.float32).astype(jnp.bfloat16),
        "mp",
        scatter_dimension=0,
        tiled=True,
    ).astype(jnp.float32)
    mixed_own = rms(h1, mlp_gain).astype(jnp.bfloat16)
    mixed = lax.all_gather(mixed_own, "mp", axis=0, tiled=True)
    gate = jnp.dot(mixed, gate_full, preferred_element_type=jnp.float32)
    upper = jnp.dot(mixed, up_full, preferred_element_type=jnp.float32)
    hidden = (jax.nn.gelu(gate, approximate=True) * upper).astype(jnp.bfloat16)
    h2 = h1 + lax.psum_scatter(
        jnp.dot(hidden, down_full, preferred_element_type=jnp.float32).astype(jnp.bfloat16),
        "mp",
        scatter_dimension=0,
        tiled=True,
    ).astype(jnp.float32)
    final = rms(h2, final_gain).astype(jnp.bfloat16)
    velocity = jnp.dot(final, head_w, preferred_element_type=jnp.float32).reshape(
        own_eps, span, adim
    )
    own_target = lax.dynamic_slice_in_dim(target, first_ep, own_eps, 0)
    diff = velocity - own_target
    ep_loss = jnp.mean(diff * diff, axis=(1, 2))
    return (velocity, ep_loss)


def solution(mesh):
    in_specs = (
        P(("dp", "mp"), None, None),
        P("dp"),
        P("dp", None, None),
        P("dp", None, None),
        P("dp"),
        P(),
        P("dp", None),
        P("dp", None),
        P(),
        P(),
        P("dp", "mp"),
        P("dp", None),
        P("dp", None),
        P("mp", "dp"),
        P(),
        P("dp", "mp"),
        P("dp", "mp"),
        P("mp", "dp"),
        P(),
        P(),
    )
    out_specs = (P(("dp", "mp"), None, None), P(("dp", "mp")))
    return jax.shard_map(
        on_device, mesh=mesh, in_specs=in_specs, out_specs=out_specs, check_vma=False
    )
```

profile of v0, /device:TPU:6, one launch (start us, length us, event | category | flops | bytes accessed | tf_op | source)
XLA Modules:
  0.0 404.9 jit_solution(4263375516487390356)
XLA Ops:
  7.2 0.7 all-gather.15.cloned.1.call-update
  8.0 0.7 all-gather.17.cloned.1.call-update
  8.7 0.7 all-gather.13.cloned.1.call-update
  9.5 3.1 fusion.2
  12.5 38.1 %all-gather.15.cloned.1.call-done = bf16[2048,256]{1,0:T(8,128)(2,1)} async-done(((bf16[256,256]{1,0:T(8,128)(2,1)}), bf16[2048,256]{1,0:T(8,128)(2,1)}) %all-gather.15.cloned.1.call-update) | async-done | bytes 1048592 | tf_op jit(solution)/shard_map/all_gather | solution.py:83
  50.7 4.6 %convolution_convert_fusion.1 = bf16[1024,256]{1,0:T(8,128)(2,1)} fusion(bf16[2048,256]{1,0:T(8,128)(2,1)} %all-gather.15.cloned.1.call-done, bf16[1,1024,2048]{2,1,0:T(8,128)(2,1)} %param.20, f32[2048]{0:T(1024)S(1)} %copy-done.12, f32[1024]{0:T(1024)S(1)} %add_rsqrt_fusion), kind=kOutput, calls=%fused_computation.9 | convolution fusion | flops 1082392576 | bytes 5779456 | tf_op jit(solution)/shard_map/dot_general | solution.py:90
  55.4 36.4 %all-gather.17.cloned.1.call-done = bf16[2048,256]{1,0:T(8,128)(2,1)} async-done(((bf16[256,256]{1,0:T(8,128)(2,1)}), bf16[2048,256]{1,0:T(8,128)(2,1)}) %all-gather.17.cloned.1.call-update) | async-done | bytes 1048592 | tf_op jit(solution)/shard_map/all_gather | solution.py:84
  91.8 4.6 %convolution_convert_fusion = bf16[1024,256]{1,0:T(8,128)(2,1)} fusion(bf16[2048,256]{1,0:T(8,128)(2,1)} %all-gather.17.cloned.1.call-done, bf16[1,1024,2048]{2,1,0:T(8,128)(2,1)} %param.20, f32[2048]{0:T(1024)S(1)} %copy-done.12, f32[1024]{0:T(1024)S(1)} %add_rsqrt_fusion), kind=kOutput, calls=%fused_computation.8 | convolution fusion | flops 1082392576 | bytes 5779456 | tf_op jit(solution)/shard_map/dot_general | solution.py:95
  96.5 0.5 all-gather.19.cloned.1.call-update
  97.1 0.7 all-gather.21.cloned.1.call-update
  97.8 0.7 all-gather.23.cloned.1.call-update
  98.6 0.7 all-gather.25.cloned.1.call-update
  99.3 0.1 fusion.38
  99.5 0.5 multiply_reduce_fusion
  100.0 0.1 reshape.115
  100.2 30.9 %all_gather.41 = bf16[1024,256]{1,0:T(8,128)(2,1)S(1)} all-gather(bf16[128,256]{1,0:T(8,128)(2,1)S(1)} %copy-done.3), channel_id=1, replica_groups=mesh['dp'=8,'mp'=4] {'dp'}, dimensions={0}, use_global_device_ids=true | all-gather | bytes 589824 | tf_op jit(solution)/shard_map/all_gather | solution.py:102
  131.1 0.1 multiply_convert_fusion
  131.2 0.3 convolution_convert_fusion.5
  131.6 31.5 %all_gather.42 = bf16[1024,256]{1,0:T(8,128)(2,1)S(1)} all-gather(bf16[128,256]{1,0:T(8,128)(2,1)S(1)} %copy-done.4), channel_id=1, replica_groups=mesh['dp'=8,'mp'=4] {'dp'}, dimensions={0}, use_global_device_ids=true | all-gather | bytes 589824 | tf_op jit(solution)/shard_map/all_gather | solution.py:103
  163.1 0.3 convolution_convert_fusion.4
  163.5 1.6 fusion.10
  165.2 0.2 fusion.46
  165.5 2.5 fusion.45
  168.0 14.4 %all-gather.29.cloned.1.call-done = bf16[4096,256]{1,0:T(8,128)(2,1)} async-done(((bf16[1024,256]{1,0:T(8,128)(2,1)}), bf16[4096,256]{1,0:T(8,128)(2,1)}) %all-gather.29.cloned.1.call-update) | async-done | bytes 2097168 | tf_op jit(solution)/shard_map/all_gather | solution.py:120
  182.4 2.0 fusion.11
  184.5 0.3 fusion.9
  184.8 39.4 %all-gather.19.cloned.1.call-done = bf16[512,1024]{1,0:T(8,128)(2,1)} async-done(((bf16[512,128]{1,0:T(8,128)(2,1)}), bf16[512,1024]{1,0:T(8,128)(2,1)}) %all-gather.19.cloned.1.call-update) | async-done | bytes 1048592 | tf_op jit(solution)/shard_map/all_gather | solution.py:131
  224.2 1.6 convolution_convert_fusion.3
  225.8 10.1 %fusion = bf16[56,1024]{1,0:T(8,128)(2,1)S(1)} fusion(bf16[200,1024]{1,0:T(8,128)(2,1)S(1)} %convolution_convert_fusion.3), kind=kCustom, calls=%all-reduce-scatter | all-reduce-scatter fusion | flops 229377 | bytes 524800
  236.0 1.9 collective-permute-start
  237.9 0.6 dynamic-slice.6
  239.1 2.2 collective-permute-done
  241.4 0.2 concatenate.4
  241.6 0.2 multiply_reduce_fusion.2
  241.8 0.1 fusion.25
  241.9 6.3 %all-gather.2 = bf16[4,50,1024]{2,1,0:T(8,128)(2,1)S(1)} all-gather(bf16[1,50,1024]{2,1,0:T(8,128)(2,1)S(1)} %fusion.25), channel_id=1, replica_groups=mesh['dp'=8,'mp'=4] {'mp'}, dimensions={0}, use_global_device_ids=true | all-gather | bytes 512000 | tf_op jit(solution)/shard_map/all_gather | solution.py:145
  248.2 0.1 reshape.127
  248.3 25.8 %all-gather.21.cloned.1.call-done = bf16[1024,1024]{1,0:T(8,128)(2,1)} async-done(((bf16[128,1024]{1,0:T(8,128)(2,1)}), bf16[1024,1024]{1,0:T(8,128)(2,1)}) %all-gather.21.cloned.1.call-update) | async-done | bytes 2097168 | tf_op jit(solution)/shard_map/all_gather | solution.py:133
  274.1 2.2 fusion.47
  276.3 47.6 %all-gather.23.cloned.1.call-done = bf16[1024,1024]{1,0:T(8,128)(2,1)} async-done(((bf16[128,1024]{1,0:T(8,128)(2,1)}), bf16[1024,1024]{1,0:T(8,128)(2,1)}) %all-gather.23.cloned.1.call-update) | async-done | bytes 2097168 | tf_op jit(solution)/shard_map/all_gather | solution.py:134
  323.8 51.9 %all-gather.25.cloned.1.call-done = bf16[1024,1024]{1,0:T(8,128)(2,1)} async-done(((bf16[1024,128]{1,0:T(8,128)(2,1)}), bf16[1024,1024]{1,0:T(8,128)(2,1)}) %all-gather.25.cloned.1.call-update) | async-done | bytes 2097168 | tf_op jit(solution)/shard_map/all_gather | solution.py:136
  375.7 3.3 convolution_convert_fusion.2
  379.0 10.2 %fusion.1 = bf16[56,1024]{1,0:T(8,128)(2,1)S(1)} fusion(bf16[200,1024]{1,0:T(8,128)(2,1)S(1)} %convolution_convert_fusion.2), kind=kCustom, calls=%all-reduce-scatter.1 | all-reduce-scatter fusion | flops 229377 | bytes 524800
  389.3 1.9 collective-permute-start.1
  391.2 3.5 collective-permute-done.1
  394.7 0.2 concatenate.5
  394.9 0.2 multiply_reduce_fusion.1
  395.1 1.5 fusion.35
  (55 shorter events, 1.0 us)
Async XLA Ops:
  7.2 92.3 %copy-start = (bf16[32,1024]{1,0:T(8,128)(2,1)S(1)}, bf16[32,1024]{1,0:T(8,128)(2,1)}, u32[]{:S(2)}) copy-start(bf16[32,1024]{1,0:T(8,128)(2,1)} %param.28) | copy-start | bytes 196612
  7.2 43.5 %all-gather.15.cloned.1.call-start = ((), (), s32[]{:S(2)}) async-start(), calls=%async_computation.1 | async-start | bytes 1179648 | tf_op jit(solution)/shard_map/all_gather | solution.py:83
  7.9 83.9 %all-gather.17.cloned.1.call-start = ((), (), s32[]{:S(2)}) async-start(), calls=%async_computation.2 | async-start | bytes 1179648 | tf_op jit(solution)/shard_map/all_gather | solution.py:84
  8.7 154.9 %all-gather.13.cloned.1.call-start = ((), (), s32[]{:S(2)}) async-start(), calls=%async_computation | async-start | bytes 1179648 | tf_op jit(solution)/shard_map/all_gather | solution.py:101
  9.4 41.3 %copy-start.12 = (f32[2048]{0:T(1024)S(1)}, f32[2048]{0:T(1024)}, u32[]{:S(2)}) copy-start(f32[2048]{0:T(1024)} %param.25) | copy-start | bytes 24580
  9.4 156.1 %all-gather.27.cloned.1.call-start = ((), (), s32[]{:S(2)}) async-start(), calls=%async_computation.7 | async-start | bytes 2621440 | tf_op jit(solution)/shard_map/all_gather | solution.py:119
  55.4 43.9 %copy-start.11 = (s32[4]{0:T(128)S(1)}, s32[4]{0:T(128)}, u32[]{:S(2)}) copy-start(s32[4]{0:T(128)} %param.24) | copy-start | bytes 52
  55.4 44.1 %copy-start.1 = (f32[4,50,32]{1,2,0:T(8,128)S(1)}, f32[4,50,32]{1,2,0:T(8,128)}, u32[]{:S(2)}) copy-start(f32[4,50,32]{1,2,0:T(8,128)} %param.22) | copy-start | bytes 76804
  55.4 44.1 %copy-start.2 = (f32[4,50,32]{1,2,0:T(8,128)S(1)}, f32[4,50,32]{1,2,0:T(8,128)}, u32[]{:S(2)}) copy-start(f32[4,50,32]{1,2,0:T(8,128)} %param.23) | copy-start | bytes 76804
  55.4 127.0 %all-gather.29.cloned.1.call-start = ((), (), s32[]{:S(2)}) async-start(), calls=%async_computation.8 | async-start | bytes 2621440 | tf_op jit(solution)/shard_map/all_gather | solution.py:120
  96.4 3.8 copy-start.3
  96.5 127.8 %all-gather.19.cloned.1.call-start = ((), (), s32[]{:S(2)}) async-start(), calls=%async_computation.3 | async-start | bytes 1179648 | tf_op jit(solution)/shard_map/all_gather | solution.py:131
  97.0 34.1 %copy-start.6 = (f32[1024]{0:T(1024)S(1)}, f32[1024]{0:T(1024)}, u32[]{:S(2)}) copy-start(f32[1024]{0:T(1024)} %param.29) | copy-start | bytes 12292
  97.0 177.0 %all-gather.21.cloned.1.call-start = ((), (), s32[]{:S(2)}) async-start(), calls=%async_computation.4 | async-start | bytes 2359296 | tf_op jit(solution)/shard_map/all_gather | solution.py:133
  97.8 226.0 %all-gather.23.cloned.1.call-start = ((), (), s32[]{:S(2)}) async-start(), calls=%async_computation.5 | async-start | bytes 2359296 | tf_op jit(solution)/shard_map/all_gather | solution.py:134
  98.5 277.1 %all-gather.25.cloned.1.call-start = ((), (), s32[]{:S(2)}) async-start(), calls=%async_computation.6 | async-start | bytes 2359296 | tf_op jit(solution)/shard_map/all_gather | solution.py:136
  100.0 31.6 %copy-start.4 = (bf16[128,256]{1,0:T(8,128)(2,1)S(1)}, bf16[128,256]{1,0:T(8,128)(2,1)}, u32[]{:S(2)}) copy-start(bf16[128,256]{1,0:T(8,128)(2,1)} %param.32) | copy-start | bytes 196612
  131.1 32.4 %copy-start.9 = (s32[4]{0:T(128)S(1)}, s32[4]{0:T(128)}, u32[]{:S(2)}) copy-start(s32[4]{0:T(128)} %param.21) | copy-start | bytes 52
  184.5 53.4 %copy-start.10 = (u32[32]{0:T(128)S(1)}, u32[32]{0:T(128)}, u32[]{:S(2)}) copy-start(u32[32]{0:T(128)} %constant.63) | copy-start | bytes 388
  184.7 57.0 %copy-start.7 = (f32[1024]{0:T(1024)S(1)}, f32[1024]{0:T(1024)}, u32[]{:S(2)}) copy-start(f32[1024]{0:T(1024)} %param.34) | copy-start | bytes 12292
  236.0 5.4 %collective-permute-start = (bf16[18,1024]{1,0:T(8,128)(2,1)S(1)}, bf16[18,1024]{1,0:T(8,128)(2,1)S(1)}, u32[]{:S(2)}, u32[]{:S(2)}) collective-permute-start(bf16[18,1024]{1,0:T(8,128)(2,1)S(1)} %slice), channel_id=1, source_target_pairs={{0,1},{1,2},{2,3},{4,5},{5,6},{6,7},{8,9},{9,10},{10,11},{12,13},{... | collective-permute-start | bytes 110600
  276.2 118.9 %copy-start.5 = (bf16[1024,32]{0,1:T(8,128)(2,1)S(1)}, bf16[1024,32]{0,1:T(8,128)(2,1)}, u32[]{:S(2)}) copy-start(bf16[1024,32]{0,1:T(8,128)(2,1)} %param.39) | copy-start | bytes 196612
  276.3 118.9 %copy-start.8 = (f32[1024]{0:T(1024)S(1)}, f32[1024]{0:T(1024)}, u32[]{:S(2)}) copy-start(f32[1024]{0:T(1024)} %param.38) | copy-start | bytes 12292
  389.3 5.4 %collective-permute-start.1 = (bf16[18,1024]{1,0:T(8,128)(2,1)S(1)}, bf16[18,1024]{1,0:T(8,128)(2,1)S(1)}, u32[]{:S(2)}, u32[]{:S(2)}) collective-permute-start(bf16[18,1024]{1,0:T(8,128)(2,1)S(1)} %slice.1), channel_id=1, source_target_pairs={{0,1},{1,2},{2,3},{4,5},{5,6},{6,7},{8,9},{9,10},{10,11},{12,13},{... | collective-permute-start | bytes 110600
Sparse Core Ops, SparseCore 0:
  10.1 40.5 all-gather.14
  52.8 38.9 all-gather.16
  94.0 41.6 all-gather.12
  137.0 21.2 all-gather.26
  159.8 22.5 all-gather.28
  184.3 39.8 all-gather.18
  226.3 47.6 all-gather.20
  276.2 47.6 all-gather.22
  325.9 49.7 all-gather.24
where the time goes:
time: 405 us
  waiting for transfers between devices  264 us (65%)
  blocking collectives  89.1 us (22%)
  matrix products  25.5 us (6%)
  between operations  16.7 us (4%)
  starting transfers between devices  4.19 us (1%)
    all_gather x1, waiting for transfers between devices, on_device(): down_full = lax.all_gather(down_w, 'dp', axis=1, tiled=True)  51.9 us
    all_gather x1, waiting for transfers between devices, on_device(): lax.all_gather(up_w, 'dp', axis=0, tiled=True)  47.6 us
    all_gather x1, waiting for transfers between devices, on_device(): out_full = lax.all_gather(out_w, 'dp', axis=1, tiled=True)  39.4 us
    all_gather x1, waiting for transfers between devices, on_device(): lax.all_gather(key_weight, 'dp', axis=0, tiled=True)  38.1 us
    all_gather x1, waiting for transfers between devices, on_device(): lax.all_gather(value_weight, 'dp', axis=0, tiled=True)  36.4 us
    all_gather x1, blocking collectives, on_device(): lax.all_gather(avalue_w, 'dp', axis=0, tiled=True)  31.5 us
    all_gather x1, blocking collectives, on_device(): lax.all_gather(akey_w, 'dp', axis=0, tiled=True)  30.9 us
    all_gather x1, waiting for transfers between devices, on_device(): lax.all_gather(gate_w, 'dp', axis=0, tiled=True)  25.8 us
  transfers between devices with their start and end apart: 11, of which 9 were waited for; matrix products, arithmetic and copies ran while one was open for 9% of the time, Pallas kernels for 0%

commit v1 on v0

--- a/solution.py
+++ b/solution.py
@@ -128,7 +128,7 @@
         prefix_len,
     )
     attn = attn.reshape(rows_total, local_heads * head_size)
-    out_full = lax.all_gather(out_w, "dp", axis=1, tiled=True)
+    out_full = jnp.concatenate(lax.all_gather(out_w, axis_name="dp"), axis=1)
     gate_full, up_full = (
         lax.all_gather(gate_w, "dp", axis=0, tiled=True),
         lax.all_gather(up_w, "dp", axis=0, tiled=True),

time: 405 us -> 407 us (level)
    all_gather x1, waiting for transfers between devices: 39.4 us -> 12.2 us  [on_device(): out_full = jnp.concatenate(lax.all_gather(out_w, axis_name='dp'), axis=1)]
    all_gather x1, waiting for transfers between devices: 0.02 us -> 21 us  [on_device(): lax.all_gather(pkeys, 'mp', axis=0, tiled=True)]
    all_gather x1, waiting for transfers between devices: 14.4 us -> 21.5 us  [on_device(): lax.all_gather(pvals, 'mp', axis=0, tiled=True)]
  transfers between devices with their start and end apart: 11 -> 11, of which waited for: 9 -> 10; matrix products, arithmetic and copies ran while one was open for 9% -> 9% of each run, Pallas kernels for 0% -> 0%
where the time goes in v1:
time: 407 us; the launch traced here: 406 us
  waiting for transfers between devices  264 us (65%)
  blocking collectives  90.1 us (22%)
  matrix products  24.3 us (6%)
  between operations  16.7 us (4%)
  starting transfers between devices  4.19 us (1%)
    all_gather x1, waiting for transfers between devices, on_device(): down_full = lax.all_gather(down_w, 'dp', axis=1, tiled=True)  51.9 us
    all_gather x1, waiting for transfers between devices, on_device(): lax.all_gather(up_w, 'dp', axis=0, tiled=True)  47.6 us
    all_gather x1, waiting for transfers between devices, on_device(): lax.all_gather(key_weight, 'dp', axis=0, tiled=True)  37.6 us
    all_gather x1, waiting for transfers between devices, on_device(): lax.all_gather(value_weight, 'dp', axis=0, tiled=True)  36.4 us
    all_gather x1, blocking collectives, on_device(): lax.all_gather(avalue_w, 'dp', axis=0, tiled=True)  31.8 us
    all_gather x1, blocking collectives, on_device(): lax.all_gather(akey_w, 'dp', axis=0, tiled=True)  31.1 us
    all_gather x1, waiting for transfers between devices, on_device(): lax.all_gather(gate_w, 'dp', axis=0, tiled=True)  25.3 us
    all_gather x1, waiting for transfers between devices, on_device(): lax.all_gather(pvals, 'mp', axis=0, tiled=True)  21.5 us
  transfers between devices with their start and end apart: 11, of which 10 were waited for; matrix products, arithmetic and copies ran while one was open for 9% of the time, Pallas kernels for 0%

profile of v1, /device:TPU:6, one launch (start us, length us, event | category | flops | bytes accessed | tf_op | source)
XLA Modules:
  0.0 406.2 jit_solution(4182927624271056328)
XLA Ops:
  7.2 0.7 all-gather.16.cloned.1.call-update
  8.0 0.7 all-gather.18.cloned.1.call-update
  8.7 0.7 all-gather.14.cloned.1.call-update
  9.4 0.5 all-gather.30.cloned.1.call-update
  10.0 3.1 fusion.2
  13.1 37.6 %all-gather.16.cloned.1.call-done = bf16[2048,256]{1,0:T(8,128)(2,1)} async-done(((bf16[256,256]{1,0:T(8,128)(2,1)}), bf16[2048,256]{1,0:T(8,128)(2,1)}) %all-gather.16.cloned.1.call-update) | async-done | bytes 1048592 | tf_op jit(solution)/shard_map/all_gather | solution.py:83
  50.7 4.6 %convolution_convert_fusion.1 = bf16[1024,256]{1,0:T(8,128)(2,1)} fusion(bf16[2048,256]{1,0:T(8,128)(2,1)} %all-gather.16.cloned.1.call-done, bf16[1,1024,2048]{2,1,0:T(8,128)(2,1)} %param.20, f32[2048]{0:T(1024)S(1)} %copy-done.12, f32[1024]{0:T(1024)S(1)} %add_rsqrt_fusion), kind=kOutput, calls=%fused_computation.9 | convolution fusion | flops 1082392576 | bytes 5779456 | tf_op jit(solution)/shard_map/dot_general | solution.py:90
  55.4 36.4 %all-gather.18.cloned.1.call-done = bf16[2048,256]{1,0:T(8,128)(2,1)} async-done(((bf16[256,256]{1,0:T(8,128)(2,1)}), bf16[2048,256]{1,0:T(8,128)(2,1)}) %all-gather.18.cloned.1.call-update) | async-done | bytes 1048592 | tf_op jit(solution)/shard_map/all_gather | solution.py:84
  91.8 4.6 %convolution_convert_fusion = bf16[1024,256]{1,0:T(8,128)(2,1)} fusion(bf16[2048,256]{1,0:T(8,128)(2,1)} %all-gather.18.cloned.1.call-done, bf16[1,1024,2048]{2,1,0:T(8,128)(2,1)} %param.20, f32[2048]{0:T(1024)S(1)} %copy-done.12, f32[1024]{0:T(1024)S(1)} %add_rsqrt_fusion), kind=kOutput, calls=%fused_computation.8 | convolution fusion | flops 1082392576 | bytes 5779456 | tf_op jit(solution)/shard_map/dot_general | solution.py:95
  96.5 0.7 all-gather.20.cloned.1.call-update
  97.3 0.7 all-gather.22.cloned.1.call-update
  98.0 0.7 all-gather.24.cloned.1.call-update
  98.7 0.1 fusion.38
  98.9 0.5 multiply_reduce_fusion
  99.6 31.1 %all_gather.44 = bf16[1024,256]{1,0:T(8,128)(2,1)S(1)} all-gather(bf16[128,256]{1,0:T(8,128)(2,1)S(1)} %copy-done.3), channel_id=1, replica_groups=mesh['dp'=8,'mp'=4] {'dp'}, dimensions={0}, use_global_device_ids=true | all-gather | bytes 589824 | tf_op jit(solution)/shard_map/all_gather | solution.py:102
  130.7 0.1 multiply_convert_fusion
  130.8 0.3 convolution_convert_fusion.5
  131.2 31.8 %all_gather.45 = bf16[1024,256]{1,0:T(8,128)(2,1)S(1)} all-gather(bf16[128,256]{1,0:T(8,128)(2,1)S(1)} %copy-done.4), channel_id=1, replica_groups=mesh['dp'=8,'mp'=4] {'dp'}, dimensions={0}, use_global_device_ids=true | all-gather | bytes 589824 | tf_op jit(solution)/shard_map/all_gather | solution.py:103
  163.0 0.3 convolution_convert_fusion.4
  163.4 1.6 fusion.10
  165.1 12.2 %all-gather.30.cloned.1.call-done = bf16[4096,128]{1,0:T(8,128)(2,1)} async-done(((bf16[512,128]{1,0:T(8,128)(2,1)}), bf16[4096,128]{1,0:T(8,128)(2,1)}) %all-gather.30.cloned.1.call-update) | async-done | bytes 1048592 | tf_op jit(solution)/shard_map/all_gather | solution.py:131
  177.4 1.5 copy.23
  178.8 0.2 fusion.46
  179.1 21.0 %all-gather.26.cloned.1.call-done = bf16[4096,256]{1,0:T(8,128)(2,1)} async-done(((bf16[1024,256]{1,0:T(8,128)(2,1)}), bf16[4096,256]{1,0:T(8,128)(2,1)}) %all-gather.26.cloned.1.call-update) | async-done | bytes 2097168 | tf_op jit(solution)/shard_map/all_gather | solution.py:119
  200.1 2.5 fusion.45
  202.5 21.5 %all-gather.28.cloned.1.call-done = bf16[4096,256]{1,0:T(8,128)(2,1)} async-done(((bf16[1024,256]{1,0:T(8,128)(2,1)}), bf16[4096,256]{1,0:T(8,128)(2,1)}) %all-gather.28.cloned.1.call-update) | async-done | bytes 2097168 | tf_op jit(solution)/shard_map/all_gather | solution.py:120
  224.1 2.0 fusion.11
  226.1 0.3 fusion.9
  226.5 0.5 convolution_convert_fusion.3
  227.0 10.6 %fusion = bf16[56,1024]{1,0:T(8,128)(2,1)S(1)} fusion(bf16[200,1024]{1,0:T(8,128)(2,1)S(1)} %convolution_convert_fusion.3), kind=kCustom, calls=%all-reduce-scatter | all-reduce-scatter fusion | flops 229377 | bytes 524800
  237.7 1.9 collective-permute-start
  239.6 0.6 dynamic-slice.6
  240.9 2.2 collective-permute-done
  243.1 0.2 concatenate.4
  243.3 0.2 multiply_reduce_fusion.2
  243.6 6.3 %all-gather.3 = bf16[4,50,1024]{2,1,0:T(8,128)(2,1)S(1)} all-gather(bf16[1,50,1024]{2,1,0:T(8,128)(2,1)S(1)} %fusion.25), channel_id=1, replica_groups=mesh['dp'=8,'mp'=4] {'mp'}, dimensions={0}, use_global_device_ids=true | all-gather | bytes 512000 | tf_op jit(solution)/shard_map/all_gather | solution.py:145
  249.9 0.1 reshape.136
  250.0 25.3 %all-gather.20.cloned.1.call-done = bf16[1024,1024]{1,0:T(8,128)(2,1)} async-done(((bf16[128,1024]{1,0:T(8,128)(2,1)}), bf16[1024,1024]{1,0:T(8,128)(2,1)}) %all-gather.20.cloned.1.call-update) | async-done | bytes 2097168 | tf_op jit(solution)/shard_map/all_gather | solution.py:133
  275.3 2.2 fusion.47
  277.5 47.6 %all-gather.22.cloned.1.call-done = bf16[1024,1024]{1,0:T(8,128)(2,1)} async-done(((bf16[128,1024]{1,0:T(8,128)(2,1)}), bf16[1024,1024]{1,0:T(8,128)(2,1)}) %all-gather.22.cloned.1.call-update) | async-done | bytes 2097168 | tf_op jit(solution)/shard_map/all_gather | solution.py:134
  325.1 51.9 %all-gather.24.cloned.1.call-done = bf16[1024,1024]{1,0:T(8,128)(2,1)} async-done(((bf16[1024,128]{1,0:T(8,128)(2,1)}), bf16[1024,1024]{1,0:T(8,128)(2,1)}) %all-gather.24.cloned.1.call-update) | async-done | bytes 2097168 | tf_op jit(solution)/shard_map/all_gather | solution.py:136
  377.0 3.3 convolution_convert_fusion.2
  380.3 10.2 %fusion.1 = bf16[56,1024]{1,0:T(8,128)(2,1)S(1)} fusion(bf16[200,1024]{1,0:T(8,128)(2,1)S(1)} %convolution_convert_fusion.2), kind=kCustom, calls=%all-reduce-scatter.1 | all-reduce-scatter fusion | flops 229377 | bytes 524800
  390.6 1.9 collective-permute-start.1
  392.5 3.5 collective-permute-done.1
  396.0 0.2 concatenate.5
  396.2 0.2 multiply_reduce_fusion.1
  396.4 1.5 fusion.35
  (56 shorter events, 1.2 us)
Async XLA Ops:
  7.2 91.7 %copy-start = (bf16[32,1024]{1,0:T(8,128)(2,1)S(1)}, bf16[32,1024]{1,0:T(8,128)(2,1)}, u32[]{:S(2)}) copy-start(bf16[32,1024]{1,0:T(8,128)(2,1)} %param.28) | copy-start | bytes 196612
  7.2 43.5 %all-gather.16.cloned.1.call-start = ((), (), s32[]{:S(2)}) async-start(), calls=%async_computation.1 | async-start | bytes 1179648 | tf_op jit(solution)/shard_map/all_gather | solution.py:83
  7.9 83.9 %all-gather.18.cloned.1.call-start = ((), (), s32[]{:S(2)}) async-start(), calls=%async_computation.2 | async-start | bytes 1179648 | tf_op jit(solution)/shard_map/all_gather | solution.py:84
  8.7 154.7 %all-gather.14.cloned.1.call-start = ((), (), s32[]{:S(2)}) async-start(), calls=%async_computation | async-start | bytes 1179648 | tf_op jit(solution)/shard_map/all_gather | solution.py:101
  9.4 168.0 %all-gather.30.cloned.1.call-start = ((), (), s32[]{:S(2)}) async-start(), calls=%async_computation.8 | async-start | bytes 1179648 | tf_op jit(solution)/shard_map/all_gather | solution.py:131
  10.0 40.7 %copy-start.12 = (f32[2048]{0:T(1024)S(1)}, f32[2048]{0:T(1024)}, u32[]{:S(2)}) copy-start(f32[2048]{0:T(1024)} %param.25) | copy-start | bytes 24580
  10.0 190.1 %all-gather.26.cloned.1.call-start = ((), (), s32[]{:S(2)}) async-start(), calls=%async_computation.6 | async-start | bytes 2621440 | tf_op jit(solution)/shard_map/all_gather | solution.py:119
  55.4 43.4 %copy-start.11 = (s32[4]{0:T(128)S(1)}, s32[4]{0:T(128)}, u32[]{:S(2)}) copy-start(s32[4]{0:T(128)} %param.24) | copy-start | bytes 52
  55.4 43.5 %copy-start.1 = (f32[4,50,32]{1,2,0:T(8,128)S(1)}, f32[4,50,32]{1,2,0:T(8,128)}, u32[]{:S(2)}) copy-start(f32[4,50,32]{1,2,0:T(8,128)} %param.22) | copy-start | bytes 76804
  55.4 43.5 %copy-start.2 = (f32[4,50,32]{1,2,0:T(8,128)S(1)}, f32[4,50,32]{1,2,0:T(8,128)}, u32[]{:S(2)}) copy-start(f32[4,50,32]{1,2,0:T(8,128)} %param.23) | copy-start | bytes 76804
  55.4 168.7 %all-gather.28.cloned.1.call-start = ((), (), s32[]{:S(2)}) async-start(), calls=%async_computation.7 | async-start | bytes 2621440 | tf_op jit(solution)/shard_map/all_gather | solution.py:120
  96.4 3.2 copy-start.3
  96.5 34.2 %copy-start.6 = (f32[1024]{0:T(1024)S(1)}, f32[1024]{0:T(1024)}, u32[]{:S(2)}) copy-start(f32[1024]{0:T(1024)} %param.29) | copy-start | bytes 12292
  96.5 178.9 %all-gather.20.cloned.1.call-start = ((), (), s32[]{:S(2)}) async-start(), calls=%async_computation.3 | async-start | bytes 2359296 | tf_op jit(solution)/shard_map/all_gather | solution.py:133
  97.2 227.9 %all-gather.22.cloned.1.call-start = ((), (), s32[]{:S(2)}) async-start(), calls=%async_computation.4 | async-start | bytes 2359296 | tf_op jit(solution)/shard_map/all_gather | solution.py:134
  98.0 279.0 %all-gather.24.cloned.1.call-start = ((), (), s32[]{:S(2)}) async-start(), calls=%async_computation.5 | async-start | bytes 2359296 | tf_op jit(solution)/shard_map/all_gather | solution.py:136
  99.4 31.8 %copy-start.4 = (bf16[128,256]{1,0:T(8,128)(2,1)S(1)}, bf16[128,256]{1,0:T(8,128)(2,1)}, u32[]{:S(2)}) copy-start(bf16[128,256]{1,0:T(8,128)(2,1)} %param.32) | copy-start | bytes 196612
  130.7 32.6 %copy-start.9 = (s32[4]{0:T(128)S(1)}, s32[4]{0:T(128)}, u32[]{:S(2)}) copy-start(s32[4]{0:T(128)} %param.21) | copy-start | bytes 52
  226.1 13.5 %copy-start.10 = (u32[32]{0:T(128)S(1)}, u32[32]{0:T(128)}, u32[]{:S(2)}) copy-start(u32[32]{0:T(128)} %constant.63) | copy-start | bytes 388
  226.4 17.1 %copy-start.7 = (f32[1024]{0:T(1024)S(1)}, f32[1024]{0:T(1024)}, u32[]{:S(2)}) copy-start(f32[1024]{0:T(1024)} %param.34) | copy-start | bytes 12292
  237.7 5.4 %collective-permute-start = (bf16[18,1024]{1,0:T(8,128)(2,1)S(1)}, bf16[18,1024]{1,0:T(8,128)(2,1)S(1)}, u32[]{:S(2)}, u32[]{:S(2)}) collective-permute-start(bf16[18,1024]{1,0:T(8,128)(2,1)S(1)} %slice), channel_id=1, source_target_pairs={{0,1},{1,2},{2,3},{4,5},{5,6},{6,7},{8,9},{9,10},{10,11},{12,13},{... | collective-permute-start | bytes 110600
  277.5 118.9 %copy-start.5 = (bf16[1024,32]{0,1:T(8,128)(2,1)S(1)}, bf16[1024,32]{0,1:T(8,128)(2,1)}, u32[]{:S(2)}) copy-start(bf16[1024,32]{0,1:T(8,128)(2,1)} %param.39) | copy-start | bytes 196612
  277.5 118.9 %copy-start.8 = (f32[1024]{0:T(1024)S(1)}, f32[1024]{0:T(1024)}, u32[]{:S(2)}) copy-start(f32[1024]{0:T(1024)} %param.38) | copy-start | bytes 12292
  390.6 5.4 %collective-permute-start.1 = (bf16[18,1024]{1,0:T(8,128)(2,1)S(1)}, bf16[18,1024]{1,0:T(8,128)(2,1)S(1)}, u32[]{:S(2)}, u32[]{:S(2)}) collective-permute-start(bf16[18,1024]{1,0:T(8,128)(2,1)S(1)} %slice.1), channel_id=1, source_target_pairs={{0,1},{1,2},{2,3},{4,5},{5,6},{6,7},{8,9},{9,10},{10,11},{12,13},{... | collective-permute-start | bytes 110600
Sparse Core Ops, SparseCore 0:
  10.1 40.5 all-gather.15
  52.8 38.9 all-gather.17
  94.0 41.6 all-gather.13
  137.7 39.6 all-gather.29
  178.8 21.2 all-gather.25
  201.5 22.5 all-gather.27
  226.2 49.0 all-gather.19
  277.4 47.6 all-gather.21
  327.1 49.7 all-gather.23
